TPU v7x, 256 devices: a 2x2x32 block of a 4x8x32 slice. The times are simulated.
256 devices in a mesh: shots: 4 (over y, x), gx: 32 (over z), gy: 2 (over core).
Axes of the slice: x: 2, y: 2, z: 32, core: 2. Of those that a mesh axis runs over, the one named last changes fastest.
The devices are a block of a 4x8x32 slice.
Arguments:
- pressure: float32 [128, 1024, 256], P(None, ('shots', 'gx'), 'gy'), parts along dimension 1, may hold values from -6 to 6
- pressure_prior: float32 [128, 1024, 256], P(None, ('shots', 'gx'), 'gy'), parts along dimension 1, may hold values from -6 to 6
- courant_square: bfloat16 [128, 256, 256], P(None, 'gx', 'gy'), may hold values from 0.049804688 to 0.1796875
- wavelet: float32 [64], P('shots'), parts along dimension 0, may hold values from -4 to 4
- delay_steps: int32 [1024, 256], P(('shots', 'gx'), 'gy'), parts along dimension 0, may hold values from 0 to 7
- source_depth: int32 [1024, 256], P(('shots', 'gx'), 'gy'), parts along dimension 0, may hold values from 4 to 31
- receiver_depth: int32 [1024, 256], P(('shots', 'gx'), 'gy'), parts along dimension 0, may hold values from 0 to 31
- receiver_field: float32 [128, 1024, 256], P(None, ('shots', 'gx'), 'gy'), parts along dimension 1, may hold values from -6 to 6
Outputs:
- pressure_final: float32 [128, 1024, 256], P(None, ('shots', 'gx'), 'gy'), parts along dimension 1
- image: float32 [128, 1024, 256], P('gx', 'shots', 'gy'), parts along dimension 1
There are 4 independent parts, one for each index of `shots`. A program takes and returns all parts, laid end to end along the dimension named above; an argument that names none is the same for every part. Nothing has to cross between parts.
All inputs are finite; a program needn't handle non-finite values.
Results may differ from a plain program's by a relative error of at most 0.00035.
Values sent between devices are 32-bit elements; how exact they have to be, the bound alone decides.
A program may use at most 64 MiB of HBM per device.

v0:
```python
import jax
import jax.numpy as jnp
from jax import lax
from jax.sharding import PartitionSpec as P

STEPS = 8


CENTER = -205.0 / 72.0
COEFS = (1.6, -0.2, 8.0 / 315.0, -1.0 / 560.0)


def padded_2(shard, sides, width):
    edges = {}
    for axis, dim in sides:
        size, length = (lax.axis_size(axis), shard.shape[dim])
        up = [(i, (i + 1) % size) for i in range(size - 1)]
        last = lax.slice_in_dim(shard, length - width, length, axis=dim)
        leading = lax.slice_in_dim(shard, 0, width, axis=dim)
        edges[dim] = (
            lax.ppermute(last, axis, up),
            lax.ppermute(leading, axis, [(b, a) for a, b in up]),
        )
    done = []
    for _, dim in sides:
        low, high = edges[dim]
        around = [(width, width) if d in done else (0, 0) for d in range(shard.ndim)]
        shard = jnp.concatenate([jnp.pad(low, around), shard, jnp.pad(high, around)], axis=dim)
        done.append(dim)
    return shard


def laplacian(field):
    depth, width, length = field.shape
    sides = padded_2(field, (("gx", 1), ("gy", 2)), 4)
    deep = jnp.pad(field, ((4, 4), (0, 0), (0, 0)))
    total = 3.0 * CENTER * field
    for k in range(1, 5):
        near = deep[4 + k : 4 + k + depth] + deep[4 - k : 4 - k + depth]
        near = (
            near
            + sides[:, 4 + k : 4 + k + width, 4 : 4 + length]
            + sides[:, 4 - k : 4 - k + width, 4 : 4 + length]
        )
        near = (
            near
            + sides[:, 4 : 4 + width, 4 + k : 4 + k + length]
            + sides[:, 4 : 4 + width, 4 - k : 4 - k + length]
        )
        total = total + COEFS[k - 1] * near
    return total


def injection(step, wavelet, delay_steps, source_depth, depth):
    picks = jnp.arange(wavelet.shape[0], dtype=jnp.int32)
    onehot = (picks[:, None, None] == (delay_steps + step)[None]).astype(jnp.float32)
    amplitude = jnp.sum(onehot * wavelet[:, None, None], axis=0)
    levels = jnp.arange(depth, dtype=jnp.int32)[:, None, None]
    return jnp.where(levels == source_depth[None], amplitude[None], jnp.zeros_like(amplitude)[None])


def depth_filter(product, padded):
    return 2.0 * product - padded[:-2] - padded[2:]


def shards(
    pressure,
    pressure_prior,
    courant_square,
    wavelet,
    delay_steps,
    source_depth,
    receiver_depth,
    receiver_field,
):
    depth = pressure.shape[0]
    coefficient = courant_square.astype(jnp.float32)
    current, prior = (pressure, pressure_prior)
    for step in range(STEPS):
        nxt = (
            2.0 * current
            - prior
            + coefficient * laplacian(current)
            + injection(step, wavelet, delay_steps, source_depth, depth)
        )
        prior, current = (current, nxt)
    levels = jnp.arange(depth, dtype=jnp.int32)[:, None, None]
    masked = jnp.where(
        levels >= receiver_depth[None], receiver_field, jnp.zeros_like(receiver_field)
    )
    product = current * masked
    rimmed = jnp.pad(product, ((1, 1), (0, 0), (0, 0)))
    filtered = depth_filter(product, rimmed)
    image = lax.all_to_all(filtered, "gx", split_axis=0, concat_axis=1, tiled=True)
    return (current, image)


def solution(mesh):
    in_specs = (
        P(None, ("shots", "gx"), "gy"),
        P(None, ("shots", "gx"), "gy"),
        P(None, "gx", "gy"),
        P("shots"),
        P(("shots", "gx"), "gy"),
        P(("shots", "gx"), "gy"),
        P(("shots", "gx"), "gy"),
        P(None, ("shots", "gx"), "gy"),
    )
    out_specs = (P(None, ("shots", "gx"), "gy"), P("gx", "shots", "gy"))
    return jax.shard_map(shards, mesh=mesh, in_specs=in_specs, out_specs=out_specs, check_vma=False)
```

profile of v0, /device:TPU:46, one launch (start us, length us, event | category | flops | bytes accessed | tf_op | source)
XLA Modules:
  0.0 235.6 jit_solution(14520718467578617591)
XLA Ops:
  0.7 1.3 fusion.273
  2.0 1.3 collective-permute-start
  3.3 4.7 %collective-permute-start.1 = (f32[128,4,128]{2,1,0:T(4,128)S(1)}, f32[128,4,128]{2,1,0:T(4,128)S(1)}, u32[]{:S(2)}, u32[]{:S(2)}) collective-permute-start(f32[128,4,128]{2,1,0:T(4,128)S(1)} %get-tuple-element.59), channel_id=1, source_target_pairs={{0,2},{2,4},{4,6},{6,8},{8,10},{10,12},{12,14},{14,16},{16,18},{18... | collective-permute-start | bytes 786440 | tf_op jit(solution)/shard_map/ppermute | solution.py:21
  8.0 1.4 fusion.272
  9.4 1.3 collective-permute-start.2
  10.8 3.1 %collective-permute-start.3 = (f32[128,8,4]{2,1,0:T(8,128)S(1)}, f32[128,8,4]{2,1,0:T(8,128)S(1)}, u32[]{:S(2)}, u32[]{:S(2)}) collective-permute-start(f32[128,8,4]{2,1,0:T(8,128)S(1)} %get-tuple-element.57), channel_id=1, source_target_pairs={{0,1},{2,3},{4,5},{6,7},{8,9},{10,11},{12,13},{14,15},{16,17},{18,... | collective-permute-start | bytes 49160 | tf_op jit(solution)/shard_map/ppermute | solution.py:21
  14.3 1.1 collective-permute-done.3
  15.4 1.4 select_maximum_fusion.15
  16.9 1.6 fusion.1
  18.5 1.3 collective-permute-start.4
  19.8 4.7 %collective-permute-start.5 = (f32[128,4,128]{2,1,0:T(4,128)S(1)}, f32[128,4,128]{2,1,0:T(4,128)S(1)}, u32[]{:S(2)}, u32[]{:S(2)}) collective-permute-start(f32[128,4,128]{2,1,0:T(4,128)S(1)} %get-tuple-element.55), channel_id=1, source_target_pairs={{0,2},{2,4},{4,6},{6,8},{8,10},{10,12},{12,14},{14,16},{16,18},{18... | collective-permute-start | bytes 786440 | tf_op jit(solution)/shard_map/ppermute | solution.py:21
  24.5 0.2 fusion.270
  24.8 1.3 collective-permute-start.6
  26.1 3.1 %collective-permute-start.7 = (f32[128,8,4]{2,1,0:T(8,128)S(1)}, f32[128,8,4]{2,1,0:T(8,128)S(1)}, u32[]{:S(2)}, u32[]{:S(2)}) collective-permute-start(f32[128,8,4]{2,1,0:T(8,128)S(1)} %get-tuple-element.53), channel_id=1, source_target_pairs={{0,1},{2,3},{4,5},{6,7},{8,9},{10,11},{12,13},{14,15},{16,17},{18,... | collective-permute-start | bytes 49160 | tf_op jit(solution)/shard_map/ppermute | solution.py:21
  29.2 1.5 collective-permute-done.7
  30.7 1.5 select_maximum_fusion.13
  32.2 1.8 fusion.3
  34.0 1.3 collective-permute-start.8
  35.4 5.0 %collective-permute-start.9 = (f32[128,4,128]{2,1,0:T(4,128)S(1)}, f32[128,4,128]{2,1,0:T(4,128)S(1)}, u32[]{:S(2)}, u32[]{:S(2)}) collective-permute-start(f32[128,4,128]{2,1,0:T(4,128)S(1)} %get-tuple-element.51), channel_id=1, source_target_pairs={{0,2},{2,4},{4,6},{6,8},{8,10},{10,12},{12,14},{14,16},{16,18},{18... | collective-permute-start | bytes 786440 | tf_op jit(solution)/shard_map/ppermute | solution.py:21
  40.6 1.3 collective-permute-start.10
  41.9 3.1 %collective-permute-start.11 = (f32[128,8,4]{2,1,0:T(8,128)S(1)}, f32[128,8,4]{2,1,0:T(8,128)S(1)}, u32[]{:S(2)}, u32[]{:S(2)}) collective-permute-start(f32[128,8,4]{2,1,0:T(8,128)S(1)} %get-tuple-element.49), channel_id=1, source_target_pairs={{0,1},{2,3},{4,5},{6,7},{8,9},{10,11},{12,13},{14,15},{16,17},{18,... | collective-permute-start | bytes 49160 | tf_op jit(solution)/shard_map/ppermute | solution.py:21
  45.0 1.5 collective-permute-done.11
  46.5 1.4 select_maximum_fusion.11
  47.9 1.8 fusion.5
  49.8 1.3 collective-permute-start.12
  51.2 5.6 %collective-permute-start.13 = (f32[128,4,128]{2,1,0:T(4,128)S(1)}, f32[128,4,128]{2,1,0:T(4,128)S(1)}, u32[]{:S(2)}, u32[]{:S(2)}) collective-permute-start(f32[128,4,128]{2,1,0:T(4,128)S(1)} %get-tuple-element.47), channel_id=1, source_target_pairs={{0,2},{2,4},{4,6},{6,8},{8,10},{10,12},{12,14},{14,16},{16,18},{18... | collective-permute-start | bytes 786440 | tf_op jit(solution)/shard_map/ppermute | solution.py:21
  57.0 1.3 collective-permute-start.14
  58.3 3.3 %collective-permute-start.15 = (f32[128,8,4]{2,1,0:T(8,128)S(1)}, f32[128,8,4]{2,1,0:T(8,128)S(1)}, u32[]{:S(2)}, u32[]{:S(2)}) collective-permute-start(f32[128,8,4]{2,1,0:T(8,128)S(1)} %get-tuple-element.45), channel_id=1, source_target_pairs={{0,1},{2,3},{4,5},{6,7},{8,9},{10,11},{12,13},{14,15},{16,17},{18,... | collective-permute-start | bytes 49160 | tf_op jit(solution)/shard_map/ppermute | solution.py:21
  61.6 1.3 collective-permute-done.15
  62.9 1.4 select_maximum_fusion.9
  64.4 1.8 fusion.7
  66.3 1.3 collective-permute-start.16
  67.6 5.8 %collective-permute-start.17 = (f32[128,4,128]{2,1,0:T(4,128)S(1)}, f32[128,4,128]{2,1,0:T(4,128)S(1)}, u32[]{:S(2)}, u32[]{:S(2)}) collective-permute-start(f32[128,4,128]{2,1,0:T(4,128)S(1)} %get-tuple-element.43), channel_id=1, source_target_pairs={{0,2},{2,4},{4,6},{6,8},{8,10},{10,12},{12,14},{14,16},{16,18},{18... | collective-permute-start | bytes 786440 | tf_op jit(solution)/shard_map/ppermute | solution.py:21
  73.4 0.2 fusion.264
  73.6 1.3 collective-permute-start.18
  74.9 3.1 %collective-permute-start.19 = (f32[128,8,4]{2,1,0:T(8,128)S(1)}, f32[128,8,4]{2,1,0:T(8,128)S(1)}, u32[]{:S(2)}, u32[]{:S(2)}) collective-permute-start(f32[128,8,4]{2,1,0:T(8,128)S(1)} %get-tuple-element.41), channel_id=1, source_target_pairs={{0,1},{2,3},{4,5},{6,7},{8,9},{10,11},{12,13},{14,15},{16,17},{18,... | collective-permute-start | bytes 49160 | tf_op jit(solution)/shard_map/ppermute | solution.py:21
  78.1 1.5 collective-permute-done.19
  79.6 1.4 select_maximum_fusion.7
  81.0 1.8 fusion.9
  82.9 1.3 collective-permute-start.20
  84.2 5.9 %collective-permute-start.21 = (f32[128,4,128]{2,1,0:T(4,128)S(1)}, f32[128,4,128]{2,1,0:T(4,128)S(1)}, u32[]{:S(2)}, u32[]{:S(2)}) collective-permute-start(f32[128,4,128]{2,1,0:T(4,128)S(1)} %get-tuple-element.39), channel_id=1, source_target_pairs={{0,2},{2,4},{4,6},{6,8},{8,10},{10,12},{12,14},{14,16},{16,18},{18... | collective-permute-start | bytes 786440 | tf_op jit(solution)/shard_map/ppermute | solution.py:21
  90.1 0.2 fusion.262
  90.3 1.3 collective-permute-start.22
  91.7 3.1 %collective-permute-start.23 = (f32[128,8,4]{2,1,0:T(8,128)S(1)}, f32[128,8,4]{2,1,0:T(8,128)S(1)}, u32[]{:S(2)}, u32[]{:S(2)}) collective-permute-start(f32[128,8,4]{2,1,0:T(8,128)S(1)} %get-tuple-element.37), channel_id=1, source_target_pairs={{0,1},{2,3},{4,5},{6,7},{8,9},{10,11},{12,13},{14,15},{16,17},{18,... | collective-permute-start | bytes 49160 | tf_op jit(solution)/shard_map/ppermute | solution.py:21
  94.8 1.5 collective-permute-done.23
  96.3 1.4 select_maximum_fusion.5
  97.7 1.8 fusion.11
  99.6 1.3 collective-permute-start.24
  100.9 5.8 %collective-permute-start.25 = (f32[128,4,128]{2,1,0:T(4,128)S(1)}, f32[128,4,128]{2,1,0:T(4,128)S(1)}, u32[]{:S(2)}, u32[]{:S(2)}) collective-permute-start(f32[128,4,128]{2,1,0:T(4,128)S(1)} %get-tuple-element.35), channel_id=1, source_target_pairs={{0,2},{2,4},{4,6},{6,8},{8,10},{10,12},{12,14},{14,16},{16,18},{18... | collective-permute-start | bytes 786440 | tf_op jit(solution)/shard_map/ppermute | solution.py:21
  107.0 1.3 collective-permute-start.26
  108.3 3.1 %collective-permute-start.27 = (f32[128,8,4]{2,1,0:T(8,128)S(1)}, f32[128,8,4]{2,1,0:T(8,128)S(1)}, u32[]{:S(2)}, u32[]{:S(2)}) collective-permute-start(f32[128,8,4]{2,1,0:T(8,128)S(1)} %get-tuple-element.33), channel_id=1, source_target_pairs={{0,1},{2,3},{4,5},{6,7},{8,9},{10,11},{12,13},{14,15},{16,17},{18,... | collective-permute-start | bytes 49160 | tf_op jit(solution)/shard_map/ppermute | solution.py:21
  111.4 1.5 collective-permute-done.27
  112.9 1.5 select_maximum_fusion.3
  114.4 1.8 fusion.13
  116.3 5.3 %collective-permute-start.29 = (f32[128,4,128]{2,1,0:T(4,128)S(1)}, f32[128,4,128]{2,1,0:T(4,128)S(1)}, u32[]{:S(2)}, u32[]{:S(2)}) collective-permute-start(f32[128,4,128]{2,1,0:T(4,128)S(1)} %get-tuple-element.30), channel_id=1, source_target_pairs={{0,2},{2,4},{4,6},{6,8},{8,10},{10,12},{12,14},{14,16},{16,18},{18... | collective-permute-start | bytes 786440 | tf_op jit(solution)/shard_map/ppermute | solution.py:21
  121.5 1.5 collective-permute-start.28
  123.3 1.3 collective-permute-start.30
  124.6 3.3 %collective-permute-start.31 = (f32[128,8,4]{2,1,0:T(8,128)S(1)}, f32[128,8,4]{2,1,0:T(8,128)S(1)}, u32[]{:S(2)}, u32[]{:S(2)}) collective-permute-start(f32[128,8,4]{2,1,0:T(8,128)S(1)} %get-tuple-element.29), channel_id=1, source_target_pairs={{0,1},{2,3},{4,5},{6,7},{8,9},{10,11},{12,13},{14,15},{16,17},{18,... | collective-permute-start | bytes 49160 | tf_op jit(solution)/shard_map/ppermute | solution.py:21
  127.9 1.5 collective-permute-done.31
  129.4 3.9 %collective-permute-done.28 = f32[128,4,128]{2,1,0:T(4,128)S(1)} collective-permute-done((f32[128,4,128]{2,1,0:T(4,128)S(1)}, f32[128,4,128]{2,1,0:T(4,128)S(1)}, u32[]{:S(2)}, u32[]{:S(2)}) %collective-permute-start.28) | collective-permute-done | bytes 262176 | tf_op jit(solution)/shard_map/ppermute | solution.py:22
  133.2 1.4 select_maximum_fusion.1
  134.7 2.6 %select_multiply_fusion = (f32[128,8,128]{2,1,0:T(8,128)S(1)}, f32[128,8,128]{2,1,0:T(8,128)}) fusion(f32[128,8,128]{2,1,0:T(8,128)S(1)} %copy-done.3, s32[8,128]{1,0:T(8,128)S(1)} %copy-done.6, f32[8,128]{1,0:T(8,128)S(1)} %get-tuple-element.2, s32[8,128]{1,0:T(8,128)S(1)} %copy-done.4, f32[128,16,132]{2,1,0:T(8,128)S(1)} %get-tuple-element.13, ...), kind=kLoop, calls=%fused_computation.386 | loop fusion | flops 6291456 | bytes 7614464 | tf_op jit(solution)/shard_map/mul | solution.py:91
  137.3 97.4 %all_to_all.18 = f32[128,8,128]{2,1,0:T(8,128)S(1)} all-to-all(f32[128,8,128]{2,1,0:T(8,128)S(1)} %slice_subtract_fusion), channel_id=1, replica_groups=mesh['shots'=4,'gx'=32,'gy'=2] {'gx'}, dimensions={0} | all-to-all | bytes 1048576 | tf_op jit(solution)/shard_map/all_to_all | solution.py:94
  234.8 0.8 copy.13
  (55 shorter events, 1.8 us)
Async XLA Ops:
  0.6 13.3 %copy-start = (f32[128,8,128]{2,1,0:T(8,128)S(1)}, f32[128,8,128]{2,1,0:T(8,128)}, u32[]{:S(2)}) copy-start(f32[128,8,128]{2,1,0:T(8,128)} %param.8) | copy-start | bytes 1572868
  0.6 13.3 %copy-start.5 = (s32[8,128]{1,0:T(8,128)S(1)}, s32[8,128]{1,0:T(8,128)}, u32[]{:S(2)}) copy-start(s32[8,128]{1,0:T(8,128)} %param.12) | copy-start | bytes 12292
  0.7 13.3 %copy-start.7 = (f32[16]{0:T(128)S(1)}, f32[16]{0:T(128)}, u32[]{:S(2)}) copy-start(f32[16]{0:T(128)} %param.11) | copy-start | bytes 196
  2.0 12.1 %collective-permute-start = (f32[128,4,128]{2,1,0:T(4,128)S(1)}, f32[128,4,128]{2,1,0:T(4,128)S(1)}, u32[]{:S(2)}, u32[]{:S(2)}) collective-permute-start(f32[128,4,128]{2,1,0:T(4,128)S(1)} %get-tuple-element.58), channel_id=1, source_target_pairs={{2,0},{4,2},{6,4},{8,6},{10,8},{12,10},{14,12},{16,14},{18,16},{20... | collective-permute-start | bytes 786440 | tf_op jit(solution)/shard_map/ppermute | solution.py:22
  3.3 12.1 %collective-permute-start.1 = (f32[128,4,128]{2,1,0:T(4,128)S(1)}, f32[128,4,128]{2,1,0:T(4,128)S(1)}, u32[]{:S(2)}, u32[]{:S(2)}) collective-permute-start(f32[128,4,128]{2,1,0:T(4,128)S(1)} %get-tuple-element.59), channel_id=1, source_target_pairs={{0,2},{2,4},{4,6},{6,8},{8,10},{10,12},{12,14},{14,16},{16,18},{18... | collective-permute-start | bytes 786440 | tf_op jit(solution)/shard_map/ppermute | solution.py:21
  9.4 4.8 %collective-permute-start.2 = (f32[128,8,4]{2,1,0:T(8,128)S(1)}, f32[128,8,4]{2,1,0:T(8,128)S(1)}, u32[]{:S(2)}, u32[]{:S(2)}) collective-permute-start(f32[128,8,4]{2,1,0:T(8,128)S(1)} %get-tuple-element.56), channel_id=1, source_target_pairs={{1,0},{3,2},{5,4},{7,6},{9,8},{11,10},{13,12},{15,14},{17,16},{19,... | collective-permute-start | bytes 49160 | tf_op jit(solution)/shard_map/ppermute | solution.py:22
  10.8 4.6 %collective-permute-start.3 = (f32[128,8,4]{2,1,0:T(8,128)S(1)}, f32[128,8,4]{2,1,0:T(8,128)S(1)}, u32[]{:S(2)}, u32[]{:S(2)}) collective-permute-start(f32[128,8,4]{2,1,0:T(8,128)S(1)} %get-tuple-element.57), channel_id=1, source_target_pairs={{0,1},{2,3},{4,5},{6,7},{8,9},{10,11},{12,13},{14,15},{16,17},{18,... | collective-permute-start | bytes 49160 | tf_op jit(solution)/shard_map/ppermute | solution.py:21
  14.2 2.6 %copy-start.1 = (bf16[128,8,128]{2,1,0:T(8,128)(2,1)S(1)}, bf16[128,8,128]{2,1,0:T(8,128)(2,1)}, u32[]{:S(2)}) copy-start(bf16[128,8,128]{2,1,0:T(8,128)(2,1)} %param.10) | copy-start | bytes 786436
  14.2 2.6 %copy-start.2 = (f32[128,8,128]{2,1,0:T(8,128)S(1)}, f32[128,8,128]{2,1,0:T(8,128)}, u32[]{:S(2)}) copy-start(f32[128,8,128]{2,1,0:T(8,128)} %param.9) | copy-start | bytes 1572868
  14.2 2.6 %copy-start.4 = (s32[8,128]{1,0:T(8,128)S(1)}, s32[8,128]{1,0:T(8,128)}, u32[]{:S(2)}) copy-start(s32[8,128]{1,0:T(8,128)} %param.13) | copy-start | bytes 12292
  18.5 12.2 %collective-permute-start.4 = (f32[128,4,128]{2,1,0:T(4,128)S(1)}, f32[128,4,128]{2,1,0:T(4,128)S(1)}, u32[]{:S(2)}, u32[]{:S(2)}) collective-permute-start(f32[128,4,128]{2,1,0:T(4,128)S(1)} %get-tuple-element.54), channel_id=1, source_target_pairs={{2,0},{4,2},{6,4},{8,6},{10,8},{12,10},{14,12},{16,14},{18,16},{20... | collective-permute-start | bytes 786440 | tf_op jit(solution)/shard_map/ppermute | solution.py:22
  19.8 10.9 %collective-permute-start.5 = (f32[128,4,128]{2,1,0:T(4,128)S(1)}, f32[128,4,128]{2,1,0:T(4,128)S(1)}, u32[]{:S(2)}, u32[]{:S(2)}) collective-permute-start(f32[128,4,128]{2,1,0:T(4,128)S(1)} %get-tuple-element.55), channel_id=1, source_target_pairs={{0,2},{2,4},{4,6},{6,8},{8,10},{10,12},{12,14},{14,16},{16,18},{18... | collective-permute-start | bytes 786440 | tf_op jit(solution)/shard_map/ppermute | solution.py:21
  24.8 4.5 %collective-permute-start.6 = (f32[128,8,4]{2,1,0:T(8,128)S(1)}, f32[128,8,4]{2,1,0:T(8,128)S(1)}, u32[]{:S(2)}, u32[]{:S(2)}) collective-permute-start(f32[128,8,4]{2,1,0:T(8,128)S(1)} %get-tuple-element.52), channel_id=1, source_target_pairs={{1,0},{3,2},{5,4},{7,6},{9,8},{11,10},{13,12},{15,14},{17,16},{19,... | collective-permute-start | bytes 49160 | tf_op jit(solution)/shard_map/ppermute | solution.py:22
  26.1 4.6 %collective-permute-start.7 = (f32[128,8,4]{2,1,0:T(8,128)S(1)}, f32[128,8,4]{2,1,0:T(8,128)S(1)}, u32[]{:S(2)}, u32[]{:S(2)}) collective-permute-start(f32[128,8,4]{2,1,0:T(8,128)S(1)} %get-tuple-element.53), channel_id=1, source_target_pairs={{0,1},{2,3},{4,5},{6,7},{8,9},{10,11},{12,13},{14,15},{16,17},{18,... | collective-permute-start | bytes 49160 | tf_op jit(solution)/shard_map/ppermute | solution.py:21
  34.0 12.5 %collective-permute-start.8 = (f32[128,4,128]{2,1,0:T(4,128)S(1)}, f32[128,4,128]{2,1,0:T(4,128)S(1)}, u32[]{:S(2)}, u32[]{:S(2)}) collective-permute-start(f32[128,4,128]{2,1,0:T(4,128)S(1)} %get-tuple-element.50), channel_id=1, source_target_pairs={{2,0},{4,2},{6,4},{8,6},{10,8},{12,10},{14,12},{16,14},{18,16},{20... | collective-permute-start | bytes 786440 | tf_op jit(solution)/shard_map/ppermute | solution.py:22
  35.4 11.2 %collective-permute-start.9 = (f32[128,4,128]{2,1,0:T(4,128)S(1)}, f32[128,4,128]{2,1,0:T(4,128)S(1)}, u32[]{:S(2)}, u32[]{:S(2)}) collective-permute-start(f32[128,4,128]{2,1,0:T(4,128)S(1)} %get-tuple-element.51), channel_id=1, source_target_pairs={{0,2},{2,4},{4,6},{6,8},{8,10},{10,12},{12,14},{14,16},{16,18},{18... | collective-permute-start | bytes 786440 | tf_op jit(solution)/shard_map/ppermute | solution.py:21
  40.6 4.5 %collective-permute-start.10 = (f32[128,8,4]{2,1,0:T(8,128)S(1)}, f32[128,8,4]{2,1,0:T(8,128)S(1)}, u32[]{:S(2)}, u32[]{:S(2)}) collective-permute-start(f32[128,8,4]{2,1,0:T(8,128)S(1)} %get-tuple-element.48), channel_id=1, source_target_pairs={{1,0},{3,2},{5,4},{7,6},{9,8},{11,10},{13,12},{15,14},{17,16},{19,... | collective-permute-start | bytes 49160 | tf_op jit(solution)/shard_map/ppermute | solution.py:22
  41.9 4.6 %collective-permute-start.11 = (f32[128,8,4]{2,1,0:T(8,128)S(1)}, f32[128,8,4]{2,1,0:T(8,128)S(1)}, u32[]{:S(2)}, u32[]{:S(2)}) collective-permute-start(f32[128,8,4]{2,1,0:T(8,128)S(1)} %get-tuple-element.49), channel_id=1, source_target_pairs={{0,1},{2,3},{4,5},{6,7},{8,9},{10,11},{12,13},{14,15},{16,17},{18,... | collective-permute-start | bytes 49160 | tf_op jit(solution)/shard_map/ppermute | solution.py:21
  49.8 13.1 %collective-permute-start.12 = (f32[128,4,128]{2,1,0:T(4,128)S(1)}, f32[128,4,128]{2,1,0:T(4,128)S(1)}, u32[]{:S(2)}, u32[]{:S(2)}) collective-permute-start(f32[128,4,128]{2,1,0:T(4,128)S(1)} %get-tuple-element.46), channel_id=1, source_target_pairs={{2,0},{4,2},{6,4},{8,6},{10,8},{12,10},{14,12},{16,14},{18,16},{20... | collective-permute-start | bytes 786440 | tf_op jit(solution)/shard_map/ppermute | solution.py:22
  51.2 11.8 %collective-permute-start.13 = (f32[128,4,128]{2,1,0:T(4,128)S(1)}, f32[128,4,128]{2,1,0:T(4,128)S(1)}, u32[]{:S(2)}, u32[]{:S(2)}) collective-permute-start(f32[128,4,128]{2,1,0:T(4,128)S(1)} %get-tuple-element.47), channel_id=1, source_target_pairs={{0,2},{2,4},{4,6},{6,8},{8,10},{10,12},{12,14},{14,16},{16,18},{18... | collective-permute-start | bytes 786440 | tf_op jit(solution)/shard_map/ppermute | solution.py:21
  57.0 4.6 %collective-permute-start.14 = (f32[128,8,4]{2,1,0:T(8,128)S(1)}, f32[128,8,4]{2,1,0:T(8,128)S(1)}, u32[]{:S(2)}, u32[]{:S(2)}) collective-permute-start(f32[128,8,4]{2,1,0:T(8,128)S(1)} %get-tuple-element.44), channel_id=1, source_target_pairs={{1,0},{3,2},{5,4},{7,6},{9,8},{11,10},{13,12},{15,14},{17,16},{19,... | collective-permute-start | bytes 49160 | tf_op jit(solution)/shard_map/ppermute | solution.py:22
  58.3 4.6 %collective-permute-start.15 = (f32[128,8,4]{2,1,0:T(8,128)S(1)}, f32[128,8,4]{2,1,0:T(8,128)S(1)}, u32[]{:S(2)}, u32[]{:S(2)}) collective-permute-start(f32[128,8,4]{2,1,0:T(8,128)S(1)} %get-tuple-element.45), channel_id=1, source_target_pairs={{0,1},{2,3},{4,5},{6,7},{8,9},{10,11},{12,13},{14,15},{16,17},{18,... | collective-permute-start | bytes 49160 | tf_op jit(solution)/shard_map/ppermute | solution.py:21
  66.3 13.3 %collective-permute-start.16 = (f32[128,4,128]{2,1,0:T(4,128)S(1)}, f32[128,4,128]{2,1,0:T(4,128)S(1)}, u32[]{:S(2)}, u32[]{:S(2)}) collective-permute-start(f32[128,4,128]{2,1,0:T(4,128)S(1)} %get-tuple-element.42), channel_id=1, source_target_pairs={{2,0},{4,2},{6,4},{8,6},{10,8},{12,10},{14,12},{16,14},{18,16},{20... | collective-permute-start | bytes 786440 | tf_op jit(solution)/shard_map/ppermute | solution.py:22
  67.6 12.0 %collective-permute-start.17 = (f32[128,4,128]{2,1,0:T(4,128)S(1)}, f32[128,4,128]{2,1,0:T(4,128)S(1)}, u32[]{:S(2)}, u32[]{:S(2)}) collective-permute-start(f32[128,4,128]{2,1,0:T(4,128)S(1)} %get-tuple-element.43), channel_id=1, source_target_pairs={{0,2},{2,4},{4,6},{6,8},{8,10},{10,12},{12,14},{14,16},{16,18},{18... | collective-permute-start | bytes 786440 | tf_op jit(solution)/shard_map/ppermute | solution.py:21
  73.6 4.5 %collective-permute-start.18 = (f32[128,8,4]{2,1,0:T(8,128)S(1)}, f32[128,8,4]{2,1,0:T(8,128)S(1)}, u32[]{:S(2)}, u32[]{:S(2)}) collective-permute-start(f32[128,8,4]{2,1,0:T(8,128)S(1)} %get-tuple-element.40), channel_id=1, source_target_pairs={{1,0},{3,2},{5,4},{7,6},{9,8},{11,10},{13,12},{15,14},{17,16},{19,... | collective-permute-start | bytes 49160 | tf_op jit(solution)/shard_map/ppermute | solution.py:22
  74.9 4.6 %collective-permute-start.19 = (f32[128,8,4]{2,1,0:T(8,128)S(1)}, f32[128,8,4]{2,1,0:T(8,128)S(1)}, u32[]{:S(2)}, u32[]{:S(2)}) collective-permute-start(f32[128,8,4]{2,1,0:T(8,128)S(1)} %get-tuple-element.41), channel_id=1, source_target_pairs={{0,1},{2,3},{4,5},{6,7},{8,9},{10,11},{12,13},{14,15},{16,17},{18,... | collective-permute-start | bytes 49160 | tf_op jit(solution)/shard_map/ppermute | solution.py:21
  82.9 13.4 %collective-permute-start.20 = (f32[128,4,128]{2,1,0:T(4,128)S(1)}, f32[128,4,128]{2,1,0:T(4,128)S(1)}, u32[]{:S(2)}, u32[]{:S(2)}) collective-permute-start(f32[128,4,128]{2,1,0:T(4,128)S(1)} %get-tuple-element.38), channel_id=1, source_target_pairs={{2,0},{4,2},{6,4},{8,6},{10,8},{12,10},{14,12},{16,14},{18,16},{20... | collective-permute-start | bytes 786440 | tf_op jit(solution)/shard_map/ppermute | solution.py:22
  84.2 12.1 %collective-permute-start.21 = (f32[128,4,128]{2,1,0:T(4,128)S(1)}, f32[128,4,128]{2,1,0:T(4,128)S(1)}, u32[]{:S(2)}, u32[]{:S(2)}) collective-permute-start(f32[128,4,128]{2,1,0:T(4,128)S(1)} %get-tuple-element.39), channel_id=1, source_target_pairs={{0,2},{2,4},{4,6},{6,8},{8,10},{10,12},{12,14},{14,16},{16,18},{18... | collective-permute-start | bytes 786440 | tf_op jit(solution)/shard_map/ppermute | solution.py:21
  90.3 4.5 %collective-permute-start.22 = (f32[128,8,4]{2,1,0:T(8,128)S(1)}, f32[128,8,4]{2,1,0:T(8,128)S(1)}, u32[]{:S(2)}, u32[]{:S(2)}) collective-permute-start(f32[128,8,4]{2,1,0:T(8,128)S(1)} %get-tuple-element.36), channel_id=1, source_target_pairs={{1,0},{3,2},{5,4},{7,6},{9,8},{11,10},{13,12},{15,14},{17,16},{19,... | collective-permute-start | bytes 49160 | tf_op jit(solution)/shard_map/ppermute | solution.py:22
  91.7 4.6 %collective-permute-start.23 = (f32[128,8,4]{2,1,0:T(8,128)S(1)}, f32[128,8,4]{2,1,0:T(8,128)S(1)}, u32[]{:S(2)}, u32[]{:S(2)}) collective-permute-start(f32[128,8,4]{2,1,0:T(8,128)S(1)} %get-tuple-element.37), channel_id=1, source_target_pairs={{0,1},{2,3},{4,5},{6,7},{8,9},{10,11},{12,13},{14,15},{16,17},{18,... | collective-permute-start | bytes 49160 | tf_op jit(solution)/shard_map/ppermute | solution.py:21
  99.6 13.3 %collective-permute-start.24 = (f32[128,4,128]{2,1,0:T(4,128)S(1)}, f32[128,4,128]{2,1,0:T(4,128)S(1)}, u32[]{:S(2)}, u32[]{:S(2)}) collective-permute-start(f32[128,4,128]{2,1,0:T(4,128)S(1)} %get-tuple-element.34), channel_id=1, source_target_pairs={{2,0},{4,2},{6,4},{8,6},{10,8},{12,10},{14,12},{16,14},{18,16},{20... | collective-permute-start | bytes 786440 | tf_op jit(solution)/shard_map/ppermute | solution.py:22
  100.9 12.0 %collective-permute-start.25 = (f32[128,4,128]{2,1,0:T(4,128)S(1)}, f32[128,4,128]{2,1,0:T(4,128)S(1)}, u32[]{:S(2)}, u32[]{:S(2)}) collective-permute-start(f32[128,4,128]{2,1,0:T(4,128)S(1)} %get-tuple-element.35), channel_id=1, source_target_pairs={{0,2},{2,4},{4,6},{6,8},{8,10},{10,12},{12,14},{14,16},{16,18},{18... | collective-permute-start | bytes 786440 | tf_op jit(solution)/shard_map/ppermute | solution.py:21
  107.0 4.5 %collective-permute-start.26 = (f32[128,8,4]{2,1,0:T(8,128)S(1)}, f32[128,8,4]{2,1,0:T(8,128)S(1)}, u32[]{:S(2)}, u32[]{:S(2)}) collective-permute-start(f32[128,8,4]{2,1,0:T(8,128)S(1)} %get-tuple-element.32), channel_id=1, source_target_pairs={{1,0},{3,2},{5,4},{7,6},{9,8},{11,10},{13,12},{15,14},{17,16},{19,... | collective-permute-start | bytes 49160 | tf_op jit(solution)/shard_map/ppermute | solution.py:22
  108.3 4.6 %collective-permute-start.27 = (f32[128,8,4]{2,1,0:T(8,128)S(1)}, f32[128,8,4]{2,1,0:T(8,128)S(1)}, u32[]{:S(2)}, u32[]{:S(2)}) collective-permute-start(f32[128,8,4]{2,1,0:T(8,128)S(1)} %get-tuple-element.33), channel_id=1, source_target_pairs={{0,1},{2,3},{4,5},{6,7},{8,9},{10,11},{12,13},{14,15},{16,17},{18,... | collective-permute-start | bytes 49160 | tf_op jit(solution)/shard_map/ppermute | solution.py:21
  116.3 13.1 %collective-permute-start.29 = (f32[128,4,128]{2,1,0:T(4,128)S(1)}, f32[128,4,128]{2,1,0:T(4,128)S(1)}, u32[]{:S(2)}, u32[]{:S(2)}) collective-permute-start(f32[128,4,128]{2,1,0:T(4,128)S(1)} %get-tuple-element.30), channel_id=1, source_target_pairs={{0,2},{2,4},{4,6},{6,8},{8,10},{10,12},{12,14},{14,16},{16,18},{18... | collective-permute-start | bytes 786440 | tf_op jit(solution)/shard_map/ppermute | solution.py:21
  121.5 11.7 %collective-permute-start.28 = (f32[128,4,128]{2,1,0:T(4,128)S(1)}, f32[128,4,128]{2,1,0:T(4,128)S(1)}, u32[]{:S(2)}, u32[]{:S(2)}) collective-permute-start(f32[128,4,128]{2,1,0:T(4,128)S(1)} %get-tuple-element.31), channel_id=1, source_target_pairs={{2,0},{4,2},{6,4},{8,6},{10,8},{12,10},{14,12},{16,14},{18,16},{20... | collective-permute-start | bytes 786440 | tf_op jit(solution)/shard_map/ppermute | solution.py:22
  123.3 4.6 %collective-permute-start.30 = (f32[128,8,4]{2,1,0:T(8,128)S(1)}, f32[128,8,4]{2,1,0:T(8,128)S(1)}, u32[]{:S(2)}, u32[]{:S(2)}) collective-permute-start(f32[128,8,4]{2,1,0:T(8,128)S(1)} %get-tuple-element.28), channel_id=1, source_target_pairs={{1,0},{3,2},{5,4},{7,6},{9,8},{11,10},{13,12},{15,14},{17,16},{19,... | collective-permute-start | bytes 49160 | tf_op jit(solution)/shard_map/ppermute | solution.py:22
  124.6 10.1 %copy-start.3 = (f32[128,8,128]{2,1,0:T(8,128)S(1)}, f32[128,8,128]{2,1,0:T(8,128)}, u32[]{:S(2)}) copy-start(f32[128,8,128]{2,1,0:T(8,128)} %param.15) | copy-start | bytes 1572868
  124.6 10.1 %copy-start.6 = (s32[8,128]{1,0:T(8,128)S(1)}, s32[8,128]{1,0:T(8,128)}, u32[]{:S(2)}) copy-start(s32[8,128]{1,0:T(8,128)} %param.14) | copy-start | bytes 12292
  124.6 4.8 %collective-permute-start.31 = (f32[128,8,4]{2,1,0:T(8,128)S(1)}, f32[128,8,4]{2,1,0:T(8,128)S(1)}, u32[]{:S(2)}, u32[]{:S(2)}) collective-permute-start(f32[128,8,4]{2,1,0:T(8,128)S(1)} %get-tuple-element.29), channel_id=1, source_target_pairs={{0,1},{2,3},{4,5},{6,7},{8,9},{10,11},{12,13},{14,15},{16,17},{18,... | collective-permute-start | bytes 49160 | tf_op jit(solution)/shard_map/ppermute | solution.py:21
where the time goes:
time: 236 us
  blocking collectives  97.4 us (41%)
  starting transfers between devices  89.4 us (38%)
  other arithmetic  26.6 us (11%)
  waiting for transfers between devices  15.2 us (6%)
  local copies, waits for them, and re-layouts  5.7 us (2%)
    all_to_all x1, blocking collectives, shards(): lax.all_to_all(filtered, 'gx', split_axis=0, concat_axis=1, tiled=True)  97.4 us
    ppermute x16, starting transfers between devices, padded_2(): lax.ppermute(last, axis, up)  68.2 us
    ppermute x16, starting transfers between devices, padded_2(): lax.ppermute(leading, axis, [(b, a) for a, b in up])  21.1 us
    add x7, other arithmetic, shards(): 2.0 * current - prior + coefficient * laplacian(current)  12.4 us
    concatenate x8, other arithmetic, padded_2(): jnp.concatenate([jnp.pad(low, around), shard, jnp.pad(high, around)], axi...  11.4 us
    ppermute x16, waiting for transfers between devices, padded_2(): lax.ppermute(last, axis, up)  11.3 us
  transfers between devices with their start and end apart: 32, of which 9 were waited for; matrix products, arithmetic and copies ran while one was open for 1% of the time, Pallas kernels for 0%

commit v1 on v0

v1 whole, which is shorter than its diff:
```python
import functools

import jax
import jax.numpy as jnp
from jax import lax
from jax.experimental import pallas as pl
from jax.experimental.pallas import tpu as pltpu
from jax.sharding import PartitionSpec as P

STEPS = 8
CENTER = -205.0 / 72.0
COEFS = (1.6, -0.2, 8.0 / 315.0, -1.0 / 560.0)
REACH = 4
ROWS = 16
PAIRS = ROWS // 2
MESH = pl.DeviceIdType.MESH


def kernel(
    ring,
    pressure, prior, courant, wavelet, delay, source, receiver, snapshot,
    final, image,
    field, courant_in, courant_f32, samples, delay_v, source_v, receiver_v, snapshot_v,
    amplitude, product, filtered,
    to_left, to_right, from_left, from_right, side,
    load_sem, left_send, right_send, side_send, left_recv, right_recv, side_recv,
    image_send, image_recv, out_sem, token_left, token_right,
):
    depth, width, lanes = pressure.shape
    chunks = depth // ROWS
    slab = depth // ring
    me, my_y = lax.axis_index("gx"), lax.axis_index("gy")
    right, left = lax.rem(me + 1, ring), lax.rem(me + ring - 1, ring)
    has_left, has_right = me > 0, me < ring - 1

    inner = pl.ds(REACH, depth)
    loads = [
        pltpu.make_async_copy(src, dst, load_sem.at[i])
        for i, (src, dst) in enumerate(
            (
                (pressure, field.at[0, inner]),
                (wavelet, samples),
                (delay, delay_v),
                (source, source_v),
                (prior, field.at[1, inner]),
                (courant, courant_in),
                (receiver, receiver_v),
                (snapshot, snapshot_v),
            )
        )
    ]
    for load in loads:
        load.start()

    barrier = pltpu.get_barrier_semaphore()
    for peer in ({"gx": left}, {"gx": right}, {"gy": 1 - my_y}):
        pl.semaphore_signal(barrier, inc=1, device_id=peer, device_id_type=MESH)

    zero = jnp.zeros((width, lanes), jnp.float32)
    for half in range(2):
        for i in range(REACH):
            field[half, i] = zero
            field[half, depth + REACH + i] = zero
    product[0] = zero
    product[depth + 1] = zero

    @pl.when(jnp.logical_not(has_left))
    def _():
        from_left[...] = jnp.zeros_like(from_left)

    @pl.when(jnp.logical_not(has_right))
    def _():
        from_right[...] = jnp.zeros_like(from_right)

    sub = lax.broadcasted_iota(jnp.int32, (width, lanes), 0)
    lane = lax.broadcasted_iota(jnp.int32, (width, lanes), 1)
    low = sub < REACH
    facing = (lane // (lanes // 2)) == my_y

    def left_copy(slot, c):
        return pltpu.make_async_remote_copy(
            to_left.at[slot, c], from_right.at[slot, c], left_send.at[slot, c],
            right_recv.at[slot, c], device_id={"gx": left}, device_id_type=MESH,
        )

    def right_copy(slot, c):
        return pltpu.make_async_remote_copy(
            to_right.at[slot, c], from_left.at[slot, c], right_send.at[slot, c],
            left_recv.at[slot, c], device_id={"gx": right}, device_id_type=MESH,
        )

    def side_copy(slot, c):
        return pltpu.make_async_remote_copy(
            field.at[slot, pl.ds(REACH + c * ROWS, ROWS)], side.at[slot, pl.ds(c * ROWS, ROWS)],
            side_send.at[slot, c], side_recv.at[slot, c],
            device_id={"gy": 1 - my_y}, device_id_type=MESH,
        )

    def send(slot, c):
        @pl.when(has_left)
        def _():
            left_copy(slot, c).start()

        @pl.when(has_right)
        def _():
            right_copy(slot, c).start()

        side_copy(slot, c).start()

    def sent(slot, c):
        @pl.when(has_left)
        def _():
            left_copy(slot, c).wait_send()

        @pl.when(has_right)
        def _():
            right_copy(slot, c).wait_send()

        side_copy(slot, c).wait_send()

    def arrived(slot, c):
        @pl.when(has_left)
        def _():
            right_copy(slot, c).wait_recv()

        @pl.when(has_right)
        def _():
            left_copy(slot, c).wait_recv()

        side_copy(slot, c).wait_recv()

    def pack(slot, c, i, first, second):
        turned = pltpu.roll(second, REACH, 0)
        to_left[slot, c, i] = jnp.where(low, first, turned)
        to_right[slot, c, i] = jnp.where(low, turned, first)

    def rounds(c):
        @pl.when(lax.rem(c, 4) == 0)
        def _():
            pl.semaphore_signal(token_right, inc=1, device_id={"gx": left}, device_id_type=MESH)
            pl.semaphore_signal(token_left, inc=1, device_id={"gx": right}, device_id_type=MESH)

        @pl.when(lax.rem(c, 4) == 3)
        def _():
            pl.semaphore_wait(token_left, 1)
            pl.semaphore_wait(token_right, 1)

    def advanced(now, later, c, z, halo, amp, where_from):
        at = z + REACH
        mine = field[now, at]
        beside = jnp.where(facing, side[now, z], 0.0)
        total = (3.0 * CENTER) * mine
        for k in range(1, REACH + 1):
            near = field[now, at + k] + field[now, at - k]
            if k == REACH:
                near = near + pltpu.roll(mine + halo, k, 0)
            else:
                near = near + pltpu.roll(jnp.where(sub >= k, mine, halo), width - k, 0)
                near = near + pltpu.roll(jnp.where(sub < width - k, mine, halo), k, 0)
            near = near + pltpu.roll(jnp.where(lane >= k, mine, beside), lanes - k, 1)
            near = near + pltpu.roll(jnp.where(lane < lanes - k, mine, beside), k, 1)
            total = total + COEFS[k - 1] * near
        added = jnp.where(where_from == z, amp, 0.0)
        return 2.0 * mine - field[later, at] + courant_f32[z] * total + added

    def halos(now, c, i):
        a, b = from_left[now, c, i], from_right[now, c, i]
        return jnp.where(low, b, a), pltpu.roll(jnp.where(low, a, b), REACH, 0)

    loads[0].wait()
    pl.semaphore_wait(barrier, 3)

    def open_chunk(c, _):
        for i in range(PAIRS):
            z = c * ROWS + 2 * i + REACH
            pack(0, c, i, field[0, z], field[0, z + 1])
        send(0, c)
        return 0

    lax.fori_loop(0, chunks, open_chunk, 0)

    for load in loads[1:]:
        load.wait()
    when = delay_v[...]
    for t in range(STEPS):
        amp = jnp.zeros((width, lanes), jnp.float32)
        for pick in range(samples.shape[0]):
            amp = amp + jnp.where(when + t == pick, samples[pick], 0.0)
        amplitude[t] = amp

    def widen(c, _):
        for i in range(ROWS):
            courant_f32[c * ROWS + i] = courant_in[c * ROWS + i].astype(jnp.float32)
        return 0

    lax.fori_loop(0, chunks, widen, 0)

    def step(t, _):
        now, later = lax.rem(t, 2), lax.rem(t + 1, 2)

        def chunk(c, _):
            rounds(c)
            arrived(now, c)

            @pl.when(t > 0)
            def _():
                sent(later, c)

            amp, where_from = amplitude[t], source_v[...]
            for i in range(PAIRS):
                z = c * ROWS + 2 * i
                new = [
                    advanced(now, later, c, z + j, halo, amp, where_from)
                    for j, halo in enumerate(halos(now, c, i))
                ]
                field[later, z + REACH] = new[0]
                field[later, z + REACH + 1] = new[1]
                pack(later, c, i, *new)
            send(later, c)
            return 0

        lax.fori_loop(0, chunks, chunk, 0)
        return 0

    lax.fori_loop(0, STEPS - 1, step, 0)

    now, later = (STEPS - 1) % 2, STEPS % 2

    def last_chunk(c, _):
        rounds(c)
        arrived(now, c)
        sent(later, c)
        amp, where_from, first_level = amplitude[STEPS - 1], source_v[...], receiver_v[...]
        for i in range(PAIRS):
            for j, halo in enumerate(halos(now, c, i)):
                z = c * ROWS + 2 * i + j
                new = advanced(now, later, c, z, halo, amp, where_from)
                field[later, z + REACH] = new
                product[z + 1] = new * jnp.where(first_level <= z, snapshot_v[z], 0.0)
        return 0

    lax.fori_loop(0, chunks, last_chunk, 0)

    keep = pltpu.make_async_copy(field.at[later, inner], final, out_sem.at[0])

    def image_chunk(c, _):
        for i in range(ROWS):
            z = c * ROWS + i
            filtered[z] = 2.0 * product[z + 1] - product[z] - product[z + 2]
        return 0

    lax.fori_loop(0, chunks, image_chunk, 0)

    def block(owner):
        return filtered.at[pl.ds(owner * slab, slab)]

    def place(owner):
        return image.at[:, pl.ds(pl.multiple_of(owner * width, width), width), :]

    def image_copy(owner):
        return pltpu.make_async_remote_copy(
            block(owner), place(me), image_send.at[owner], image_recv.at[me],
            device_id={"gx": owner}, device_id_type=MESH,
        )

    def image_in(origin):
        return pltpu.make_async_remote_copy(
            block(origin), place(origin), image_send.at[origin], image_recv.at[origin],
            device_id={"gx": origin}, device_id_type=MESH,
        )

    half = ring // 2
    image_copy(lax.rem(me + half, ring)).start()

    def spread(i, _):
        k = half - 1 - i
        image_copy(lax.rem(me + k, ring)).start()
        image_copy(lax.rem(me + ring - k, ring)).start()
        return 0

    lax.fori_loop(0, half - 1, spread, 0)
    own = pltpu.make_async_copy(block(me), place(me), out_sem.at[1])
    own.start()
    keep.start()

    def drain(c, _):
        sent(now, c)
        return 0

    lax.fori_loop(0, chunks, drain, 0)
    own.wait()
    keep.wait()

    def collect(i, _):
        other = lax.rem(me + 1 + i, ring)
        image_in(other).wait_recv()
        image_copy(other).wait_send()
        return 0

    lax.fori_loop(0, ring - 1, collect, 0)


def shards(ring, *args):
    pressure = args[0]
    depth, width, lanes = pressure.shape
    chunks, slab = depth // ROWS, depth // ring
    tile = (width, lanes)
    f32 = jnp.float32
    packets = pltpu.VMEM((2, chunks, PAIRS) + tile, f32)
    dma = pltpu.SemaphoreType.DMA
    return pl.pallas_call(
        functools.partial(kernel, ring),
        out_shape=(
            jax.ShapeDtypeStruct((depth,) + tile, f32),
            jax.ShapeDtypeStruct((slab, ring * width, lanes), f32),
        ),
        in_specs=[pl.BlockSpec(memory_space=pl.ANY)] * 8,
        out_specs=[pl.BlockSpec(memory_space=pl.ANY)] * 2,
        scratch_shapes=[
            pltpu.VMEM((2, depth + 2 * REACH) + tile, f32),
            pltpu.VMEM((depth,) + tile, jnp.bfloat16),
            pltpu.VMEM((depth,) + tile, f32),
            pltpu.SMEM(args[3].shape, f32),
            pltpu.VMEM(tile, jnp.int32),
            pltpu.VMEM(tile, jnp.int32),
            pltpu.VMEM(tile, jnp.int32),
            pltpu.VMEM((depth,) + tile, f32),
            pltpu.VMEM((STEPS,) + tile, f32),
            pltpu.VMEM((depth + 2,) + tile, f32),
            pltpu.VMEM((depth,) + tile, f32),
            packets, packets, packets, packets,
            pltpu.VMEM((2, depth) + tile, f32),
            dma((8,)),
            dma((2, chunks)), dma((2, chunks)), dma((2, chunks)),
            dma((2, chunks)), dma((2, chunks)), dma((2, chunks)),
            dma((ring,)), dma((ring,)), dma((2,)),
            pltpu.SemaphoreType.REGULAR, pltpu.SemaphoreType.REGULAR,
        ],
        compiler_params=pltpu.CompilerParams(collective_id=0, has_side_effects=True),
        name="march",
    )(*args)


def solution(mesh):
    in_specs = (
        P(None, ("shots", "gx"), "gy"),
        P(None, ("shots", "gx"), "gy"),
        P(None, "gx", "gy"),
        P("shots"),
        P(("shots", "gx"), "gy"),
        P(("shots", "gx"), "gy"),
        P(("shots", "gx"), "gy"),
        P(None, ("shots", "gx"), "gy"),
    )
    out_specs = (P(None, ("shots", "gx"), "gy"), P("gx", "shots", "gy"))
    return jax.shard_map(
        functools.partial(shards, mesh.shape["gx"]),
        mesh=mesh, in_specs=in_specs, out_specs=out_specs, check_vma=False,
    )
```

time: 236 us -> 127 us (0.54)
  Pallas kernels: 0 us -> 123 us
  blocking collectives: 97.4 us -> 0 us
  starting transfers between devices: 89.4 us -> 0 us
  other arithmetic: 26.6 us -> 0 us
  waiting for transfers between devices: 15.2 us -> 0 us
  local copies, waits for them, and re-layouts: 5.7 us -> 2.72 us
    pallas_call x0 -> x1, Pallas kernels: none -> 123 us  [shards(): pl.pallas_call(functools.partial(kernel, ring), out_shape=(jax.ShapeDtype...]
    all_to_all x1 -> x0, blocking collectives: 97.4 us -> none  [shards(): lax.all_to_all(filtered, 'gx', split_axis=0, concat_axis=1, tiled=True)]
    ppermute x32 -> x0, starting transfers between devices: 89.4 us -> none  [the longest x16 68.2 us: padded_2(): lax.ppermute(last, axis, up)]
    ppermute x32 -> x0, waiting for transfers between devices: 15.2 us -> none  [the longest x16 11.3 us: padded_2(): lax.ppermute(last, axis, up)]
    add x8 -> x0, other arithmetic: 12.4 us -> none  [the longest x7 12.4 us: shards(): 2.0 * current - prior + coefficient * laplacian(current)]
    concatenate x8 -> x0, other arithmetic: 11.4 us -> none  [padded_2(): jnp.concatenate([jnp.pad(low, around), shard, jnp.pad(high, around)], axi...]
    slice x16 -> x0, local copies, waits for them, and re-layouts: 4.73 us -> none  [the longest x15 4.64 us: padded_2(): leading = lax.slice_in_dim(shard, 0, width, axis=dim)]
    unnamed x17 -> x4, local copies, waits for them, and re-layouts: 0.08 us -> 2.72 us
  transfers between devices with their start and end apart: 32 -> 0, of which waited for: 9 -> 0; matrix products, arithmetic and copies ran while one was open for 1% -> 0% of each run, Pallas kernels for 0% -> 0%
where the time goes in v1:
time: 127 us
  Pallas kernels  123 us (97%)
  local copies, waits for them, and re-layouts  2.72 us (2%)
    pallas_call x1, Pallas kernels, shards(): pl.pallas_call(functools.partial(kernel, ring), out_shape=(jax.ShapeDtype...  123 us
    unnamed x4, local copies, waits for them, and re-layouts  2.72 us

profile of v1, /device:TPU:46, one launch (start us, length us, event | category | flops | bytes accessed | tf_op | source)
XLA Modules:
  0.0 126.8 jit_solution(16526845562538582287)
XLA Ops:
  0.6 123.4 %march.1 = (f32[128,8,128]{2,1,0:T(8,128)}, f32[4,256,128]{2,1,0:T(8,128)}) custom-call(f32[128,8,128]{2,1,0:T(8,128)} %pressure.1, f32[128,8,128]{2,1,0:T(8,128)} %prior.1, bf16[128,8,128]{2,1,0:T(8,128)(2,1)} %courant.1, f32[16]{0:T(128)} %wavelet.1, s32[8,128]{1,0:T(8,128)} %delay.1, s32[8,128]{1,0:T(8,128)} %source.1, s32[8,128]{1,0:T(8,128)} %receiver.1, ...), custom_call_target="tpu_custom_call" | custom-call | tf_op jit(solution)/shard_map/march/pallas_call | solution.py:311
  124.1 0.0 copy-start
  124.1 1.9 %copy.12 = f32[128,8,128]{2,1,0:T(8,128)} copy(f32[128,8,128]{2,1,0:T(8,128)} %get-tuple-element.4) | data formatting | bytes 1048576
  126.0 0.0 copy-done
  126.0 0.8 copy.13
Async XLA Ops:
  124.1 1.9 %copy-start = (f32[4,256,128]{2,1,0:T(8,128)S(1)}, f32[4,256,128]{2,1,0:T(8,128)}, u32[]{:S(2)}) copy-start(f32[4,256,128]{2,1,0:T(8,128)} %get-tuple-element.5) | copy-start | bytes 1572868

commit v2 on v1

--- a/solution.py
+++ b/solution.py
@@ -11,7 +11,7 @@
 CENTER = -205.0 / 72.0
 COEFS = (1.6, -0.2, 8.0 / 315.0, -1.0 / 560.0)
 REACH = 4
-ROWS = 16
+ROWS = 32
 PAIRS = ROWS // 2
 MESH = pl.DeviceIdType.MESH
 
@@ -23,7 +23,7 @@
     field, courant_in, courant_f32, samples, delay_v, source_v, receiver_v, snapshot_v,
     amplitude, product, filtered,
     to_left, to_right, from_left, from_right, side,
-    load_sem, left_send, right_send, side_send, left_recv, right_recv, side_recv,
+    chunk_sem, load_sem, left_send, right_send, side_send, left_recv, right_recv, side_recv,
     image_send, image_recv, out_sem, token_left, token_right,
 ):
     depth, width, lanes = pressure.shape
@@ -33,12 +33,23 @@
     right, left = lax.rem(me + 1, ring), lax.rem(me + ring - 1, ring)
     has_left, has_right = me > 0, me < ring - 1
 
+    barrier = pltpu.get_barrier_semaphore()
+    for peer in ({"gx": left}, {"gx": right}, {"gy": 1 - my_y}):
+        pl.semaphore_signal(barrier, inc=1, device_id=peer, device_id_type=MESH)
+
+    def load_chunk(c):
+        return pltpu.make_async_copy(
+            pressure.at[pl.ds(c * ROWS, ROWS)], field.at[0, pl.ds(REACH + c * ROWS, ROWS)],
+            chunk_sem.at[c],
+        )
+
+    for c in range(chunks):
+        load_chunk(c).start()
     inner = pl.ds(REACH, depth)
     loads = [
         pltpu.make_async_copy(src, dst, load_sem.at[i])
         for i, (src, dst) in enumerate(
             (
-                (pressure, field.at[0, inner]),
                 (wavelet, samples),
                 (delay, delay_v),
                 (source, source_v),
@@ -52,10 +63,6 @@
     for load in loads:
         load.start()
 
-    barrier = pltpu.get_barrier_semaphore()
-    for peer in ({"gx": left}, {"gx": right}, {"gy": 1 - my_y}):
-        pl.semaphore_signal(barrier, inc=1, device_id=peer, device_id_type=MESH)
-
     zero = jnp.zeros((width, lanes), jnp.float32)
     for half in range(2):
         for i in range(REACH):
@@ -135,12 +142,12 @@
         to_right[slot, c, i] = jnp.where(low, turned, first)
 
     def rounds(c):
-        @pl.when(lax.rem(c, 4) == 0)
+        @pl.when(lax.rem(c, 2) == 0)
         def _():
             pl.semaphore_signal(token_right, inc=1, device_id={"gx": left}, device_id_type=MESH)
             pl.semaphore_signal(token_left, inc=1, device_id={"gx": right}, device_id_type=MESH)
 
-        @pl.when(lax.rem(c, 4) == 3)
+        @pl.when(lax.rem(c, 2) == 1)
         def _():
             pl.semaphore_wait(token_left, 1)
             pl.semaphore_wait(token_right, 1)
@@ -167,10 +174,10 @@
         a, b = from_left[now, c, i], from_right[now, c, i]
         return jnp.where(low, b, a), pltpu.roll(jnp.where(low, a, b), REACH, 0)
 
-    loads[0].wait()
     pl.semaphore_wait(barrier, 3)
 
     def open_chunk(c, _):
+        load_chunk(c).wait()
         for i in range(PAIRS):
             z = c * ROWS + 2 * i + REACH
             pack(0, c, i, field[0, z], field[0, z + 1])
@@ -179,7 +186,7 @@
 
     lax.fori_loop(0, chunks, open_chunk, 0)
 
-    for load in loads[1:]:
+    for load in loads:
         load.wait()
     when = delay_v[...]
     for t in range(STEPS):
@@ -235,13 +242,11 @@
             for j, halo in enumerate(halos(now, c, i)):
                 z = c * ROWS + 2 * i + j
                 new = advanced(now, later, c, z, halo, amp, where_from)
-                field[later, z + REACH] = new
+                final[z] = new
                 product[z + 1] = new * jnp.where(first_level <= z, snapshot_v[z], 0.0)
         return 0
 
     lax.fori_loop(0, chunks, last_chunk, 0)
-
-    keep = pltpu.make_async_copy(field.at[later, inner], final, out_sem.at[0])
 
     def image_chunk(c, _):
         for i in range(ROWS):
@@ -259,14 +264,8 @@
 
     def image_copy(owner):
         return pltpu.make_async_remote_copy(
-            block(owner), place(me), image_send.at[owner], image_recv.at[me],
+            block(owner), place(me), image_send, image_recv,
             device_id={"gx": owner}, device_id_type=MESH,
-        )
-
-    def image_in(origin):
-        return pltpu.make_async_remote_copy(
-            block(origin), place(origin), image_send.at[origin], image_recv.at[origin],
-            device_id={"gx": origin}, device_id_type=MESH,
         )
 
     half = ring // 2
@@ -279,9 +278,8 @@
         return 0
 
     lax.fori_loop(0, half - 1, spread, 0)
-    own = pltpu.make_async_copy(block(me), place(me), out_sem.at[1])
+    own = pltpu.make_async_copy(block(me), place(me), out_sem)
     own.start()
-    keep.start()
 
     def drain(c, _):
         sent(now, c)
@@ -289,15 +287,21 @@
 
     lax.fori_loop(0, chunks, drain, 0)
     own.wait()
-    keep.wait()
-
-    def collect(i, _):
-        other = lax.rem(me + 1 + i, ring)
-        image_in(other).wait_recv()
-        image_copy(other).wait_send()
-        return 0
-
-    lax.fori_loop(0, ring - 1, collect, 0)
+
+    rest = image.at[:, pl.ds(0, (ring - 1) * width), :]
+    pltpu.make_async_copy(rest, rest, image_recv).wait()
+    pltpu.make_async_copy(rest, rest, image_send).wait()
+
+
+def put(final_in, image_in, final, image, sems):
+    copies = [
+        pltpu.make_async_copy(final_in, final, sems.at[0]),
+        pltpu.make_async_copy(image_in, image, sems.at[1]),
+    ]
+    for copy in copies:
+        copy.start()
+    for copy in copies:
+        copy.wait()
 
 
 def shards(ring, *args):
@@ -308,14 +312,12 @@
     f32 = jnp.float32
     packets = pltpu.VMEM((2, chunks, PAIRS) + tile, f32)
     dma = pltpu.SemaphoreType.DMA
-    return pl.pallas_call(
+    shapes = ((depth,) + tile, (slab, ring * width, lanes))
+    held = pl.pallas_call(
         functools.partial(kernel, ring),
-        out_shape=(
-            jax.ShapeDtypeStruct((depth,) + tile, f32),
-            jax.ShapeDtypeStruct((slab, ring * width, lanes), f32),
-        ),
+        out_shape=tuple(pltpu.VMEM(shape, f32) for shape in shapes),
         in_specs=[pl.BlockSpec(memory_space=pl.ANY)] * 8,
-        out_specs=[pl.BlockSpec(memory_space=pl.ANY)] * 2,
+        out_specs=[pl.BlockSpec(memory_space=pltpu.VMEM)] * 2,
         scratch_shapes=[
             pltpu.VMEM((2, depth + 2 * REACH) + tile, f32),
             pltpu.VMEM((depth,) + tile, jnp.bfloat16),
@@ -330,15 +332,23 @@
             pltpu.VMEM((depth,) + tile, f32),
             packets, packets, packets, packets,
             pltpu.VMEM((2, depth) + tile, f32),
-            dma((8,)),
+            dma((chunks,)), dma((7,)),
             dma((2, chunks)), dma((2, chunks)), dma((2, chunks)),
             dma((2, chunks)), dma((2, chunks)), dma((2, chunks)),
-            dma((ring,)), dma((ring,)), dma((2,)),
+            dma, dma, dma,
             pltpu.SemaphoreType.REGULAR, pltpu.SemaphoreType.REGULAR,
         ],
         compiler_params=pltpu.CompilerParams(collective_id=0, has_side_effects=True),
         name="march",
     )(*args)
+    return pl.pallas_call(
+        put,
+        out_shape=tuple(jax.ShapeDtypeStruct(shape, f32) for shape in shapes),
+        in_specs=[pl.BlockSpec(memory_space=pltpu.VMEM)] * 2,
+        out_specs=[pl.BlockSpec(memory_space=pl.ANY)] * 2,
+        scratch_shapes=[dma((2,))],
+        name="put",
+    )(*(pltpu.with_memory_space_constraint(x, pltpu.VMEM) for x in held))
 
 
 def solution(mesh):

time: 127 us -> 123 us (0.969)
  local copies, waits for them, and re-layouts: 2.72 us -> 0 us
    unnamed x4 -> x0, local copies, waits for them, and re-layouts: 2.72 us -> none
    pallas_call x1 -> x2, Pallas kernels: 123 us -> 123 us  [the longest x1 122 us: shards(): pl.pallas_call(functools.partial(kernel, ring), out_shape=tuple((pltpu.VM...]
where the time goes in v2:
time: 123 us
  Pallas kernels  123 us (100%)
    pallas_call x1, Pallas kernels, shards(): pl.pallas_call(functools.partial(kernel, ring), out_shape=tuple((pltpu.VM...  122 us

profile of v2, /device:TPU:46, one launch (start us, length us, event | category | flops | bytes accessed | tf_op | source)
XLA Modules:
  0.0 123.3 jit_solution(13292024807281376133)
XLA Ops:
  0.6 121.6 %march.1 = (f32[128,8,128]{2,1,0:T(8,128)S(1)}, f32[4,256,128]{2,1,0:T(8,128)S(1)}) custom-call(f32[128,8,128]{2,1,0:T(8,128)} %pressure.1, f32[128,8,128]{2,1,0:T(8,128)} %prior.1, bf16[128,8,128]{2,1,0:T(8,128)(2,1)} %courant.1, f32[16]{0:T(128)} %wavelet.1, s32[8,128]{1,0:T(8,128)} %delay.1, s32[8,128]{1,0:T(8,128)} %source.1, s32[8,128]{1,0:T(8,128)} %receiver.1, ...), custom_call_target="tpu_custom_call" | custom-call | tf_op jit(solution)/shard_map/march/pallas_call | solution.py:316
  122.3 1.0 put.1

commit v3 on v2

--- a/solution.py
+++ b/solution.py
@@ -13,6 +13,8 @@
 REACH = 4
 ROWS = 32
 PAIRS = ROWS // 2
+GROUP = 4
+EARLY = 10
 MESH = pl.DeviceIdType.MESH
 
 
@@ -68,8 +70,9 @@
         for i in range(REACH):
             field[half, i] = zero
             field[half, depth + REACH + i] = zero
-    product[0] = zero
-    product[depth + 1] = zero
+    for i in range(slab + 1):
+        product[i] = zero
+    product[slab + depth + 1] = zero
 
     @pl.when(jnp.logical_not(has_left))
     def _():
@@ -141,18 +144,19 @@
         to_left[slot, c, i] = jnp.where(low, first, turned)
         to_right[slot, c, i] = jnp.where(low, turned, first)
 
+    def tell():
+        pl.semaphore_signal(token_right, inc=1, device_id={"gx": left}, device_id_type=MESH)
+        pl.semaphore_signal(token_left, inc=1, device_id={"gx": right}, device_id_type=MESH)
+
+    def hear():
+        pl.semaphore_wait(token_left, 1)
+        pl.semaphore_wait(token_right, 1)
+
     def rounds(c):
-        @pl.when(lax.rem(c, 2) == 0)
-        def _():
-            pl.semaphore_signal(token_right, inc=1, device_id={"gx": left}, device_id_type=MESH)
-            pl.semaphore_signal(token_left, inc=1, device_id={"gx": right}, device_id_type=MESH)
-
-        @pl.when(lax.rem(c, 2) == 1)
-        def _():
-            pl.semaphore_wait(token_left, 1)
-            pl.semaphore_wait(token_right, 1)
-
-    def advanced(now, later, c, z, halo, amp, where_from):
+        pl.when(lax.rem(c, 2) == 0)(tell)
+        pl.when(lax.rem(c, 2) == 1)(hear)
+
+    def advanced(now, later, z, halo, amp, where_from):
         at = z + REACH
         mine = field[now, at]
         beside = jnp.where(facing, side[now, z], 0.0)
@@ -175,6 +179,7 @@
         return jnp.where(low, b, a), pltpu.roll(jnp.where(low, a, b), REACH, 0)
 
     pl.semaphore_wait(barrier, 3)
+    tell()
 
     def open_chunk(c, _):
         load_chunk(c).wait()
@@ -201,6 +206,7 @@
         return 0
 
     lax.fori_loop(0, chunks, widen, 0)
+    hear()
 
     def step(t, _):
         now, later = lax.rem(t, 2), lax.rem(t + 1, 2)
@@ -214,15 +220,19 @@
                 sent(later, c)
 
             amp, where_from = amplitude[t], source_v[...]
-            for i in range(PAIRS):
-                z = c * ROWS + 2 * i
-                new = [
-                    advanced(now, later, c, z + j, halo, amp, where_from)
-                    for j, halo in enumerate(halos(now, c, i))
+            for first in range(0, PAIRS, GROUP):
+                pairs = [
+                    [
+                        advanced(now, later, c * ROWS + 2 * i + j, halo, amp, where_from)
+                        for j, halo in enumerate(halos(now, c, i))
+                    ]
+                    for i in range(first, first + GROUP)
                 ]
-                field[later, z + REACH] = new[0]
-                field[later, z + REACH + 1] = new[1]
-                pack(later, c, i, *new)
+                for i, new in enumerate(pairs, first):
+                    z = c * ROWS + 2 * i
+                    field[later, z + REACH] = new[0]
+                    field[later, z + REACH + 1] = new[1]
+                    pack(later, c, i, *new)
             send(later, c)
             return 0
 
@@ -233,48 +243,65 @@
 
     now, later = (STEPS - 1) % 2, STEPS % 2
 
+    def block(owner):
+        return filtered.at[pl.ds(slab + owner * slab, slab)]
+
+    def place(owner):
+        return image.at[:, pl.ds(pl.multiple_of(owner * width, width), width), :]
+
+    def image_copy(owner):
+        return pltpu.make_async_remote_copy(
+            block(owner), place(me), image_send, image_recv,
+            device_id={"gx": owner}, device_id_type=MESH,
+        )
+
+    half, owners = ring // 2, ROWS // slab
+
+    def filter_row(first, count):
+        for i in range(count):
+            z = slab + first + i
+            filtered[z] = 2.0 * product[z + 1] - product[z] - product[z + 2]
+
+    def early(owner):
+        ahead = lax.rem(owner - me + ring, ring)
+        far = jnp.minimum(ahead, ring - ahead) >= EARLY
+        return far & (owner >= 0) & (owner < (chunks - 1) * owners - 1)
+
     def last_chunk(c, _):
-        rounds(c)
         arrived(now, c)
         sent(later, c)
         amp, where_from, first_level = amplitude[STEPS - 1], source_v[...], receiver_v[...]
         for i in range(PAIRS):
             for j, halo in enumerate(halos(now, c, i)):
                 z = c * ROWS + 2 * i + j
-                new = advanced(now, later, c, z, halo, amp, where_from)
+                new = advanced(now, later, z, halo, amp, where_from)
                 final[z] = new
-                product[z + 1] = new * jnp.where(first_level <= z, snapshot_v[z], 0.0)
+                product[slab + z + 1] = new * jnp.where(first_level <= z, snapshot_v[z], 0.0)
+        filter_row(c * ROWS - slab, ROWS)
+        for i in range(owners):
+            owner = c * owners - 1 + i
+
+            @pl.when(early(owner))
+            def _():
+                image_copy(owner).start()
+
         return 0
 
     lax.fori_loop(0, chunks, last_chunk, 0)
 
-    def image_chunk(c, _):
-        for i in range(ROWS):
-            z = c * ROWS + i
-            filtered[z] = 2.0 * product[z + 1] - product[z] - product[z + 2]
-        return 0
-
-    lax.fori_loop(0, chunks, image_chunk, 0)
-
-    def block(owner):
-        return filtered.at[pl.ds(owner * slab, slab)]
-
-    def place(owner):
-        return image.at[:, pl.ds(pl.multiple_of(owner * width, width), width), :]
-
-    def image_copy(owner):
-        return pltpu.make_async_remote_copy(
-            block(owner), place(me), image_send, image_recv,
-            device_id={"gx": owner}, device_id_type=MESH,
-        )
-
-    half = ring // 2
-    image_copy(lax.rem(me + half, ring)).start()
+    filter_row(depth - slab, slab)
+
+    def send_block(owner):
+        @pl.when(jnp.logical_not(early(owner)))
+        def _():
+            image_copy(owner).start()
+
+    send_block(lax.rem(me + half, ring))
 
     def spread(i, _):
         k = half - 1 - i
-        image_copy(lax.rem(me + k, ring)).start()
-        image_copy(lax.rem(me + ring - k, ring)).start()
+        send_block(lax.rem(me + k, ring))
+        send_block(lax.rem(me + ring - k, ring))
         return 0
 
     lax.fori_loop(0, half - 1, spread, 0)
@@ -328,8 +355,8 @@
             pltpu.VMEM(tile, jnp.int32),
             pltpu.VMEM((depth,) + tile, f32),
             pltpu.VMEM((STEPS,) + tile, f32),
-            pltpu.VMEM((depth + 2,) + tile, f32),
-            pltpu.VMEM((depth,) + tile, f32),
+            pltpu.VMEM((slab + depth + 2,) + tile, f32),
+            pltpu.VMEM((slab + depth,) + tile, f32),
             packets, packets, packets, packets,
             pltpu.VMEM((2, depth) + tile, f32),
             dma((chunks,)), dma((7,)),

time: 123 us -> 117 us (0.951)
  Pallas kernels: 123 us -> 117 us
    pallas_call x1, Pallas kernels: 122 us -> 116 us  [shards(): pl.pallas_call(functools.partial(kernel, ring), out_shape=tuple((pltpu.VM...]
where the time goes in v3:
time: 117 us
  Pallas kernels  117 us (100%)
    pallas_call x1, Pallas kernels, shards(): pl.pallas_call(functools.partial(kernel, ring), out_shape=tuple((pltpu.VM...  116 us

profile of v3, /device:TPU:46, one launch (start us, length us, event | category | flops | bytes accessed | tf_op | source)
XLA Modules:
  0.0 117.2 jit_solution(2234418261053834079)
XLA Ops:
  0.6 115.6 %march.1 = (f32[128,8,128]{2,1,0:T(8,128)S(1)}, f32[4,256,128]{2,1,0:T(8,128)S(1)}) custom-call(f32[128,8,128]{2,1,0:T(8,128)} %pressure.1, f32[128,8,128]{2,1,0:T(8,128)} %prior.1, bf16[128,8,128]{2,1,0:T(8,128)(2,1)} %courant.1, f32[16]{0:T(128)} %wavelet.1, s32[8,128]{1,0:T(8,128)} %delay.1, s32[8,128]{1,0:T(8,128)} %source.1, s32[8,128]{1,0:T(8,128)} %receiver.1, ...), custom_call_target="tpu_custom_call" | custom-call | tf_op jit(solution)/shard_map/march/pallas_call | solution.py:343
  116.2 1.0 put.1

commit v4 on v3

--- a/solution.py
+++ b/solution.py
@@ -15,6 +15,7 @@
 PAIRS = ROWS // 2
 GROUP = 4
 EARLY = 10
+HEAD = 6
 MESH = pl.DeviceIdType.MESH
 
 
@@ -299,12 +300,16 @@
     send_block(lax.rem(me + half, ring))
 
     def spread(i, _):
-        k = half - 1 - i
-        send_block(lax.rem(me + k, ring))
-        send_block(lax.rem(me + ring - k, ring))
-        return 0
-
-    lax.fori_loop(0, half - 1, spread, 0)
+        key = half - 1 + HEAD - i
+        for k, low_owner in ((key, False), (key - HEAD, True)):
+            for owner in (lax.rem(me + k + ring, ring), lax.rem(me - k + ring, ring)):
+                @pl.when((k >= 1) & (k < half) & ((owner < ring // 8) == low_owner))
+                def _():
+                    send_block(owner)
+
+        return 0
+
+    lax.fori_loop(0, half - 1 + HEAD, spread, 0)
     own = pltpu.make_async_copy(block(me), place(me), out_sem)
     own.start()
 

time: 117 us -> 116 us (level)
  no operation moved by 1% of the time
where the time goes in v4:
time: 116 us
  Pallas kernels  116 us (100%)
    pallas_call x1, Pallas kernels, shards(): pl.pallas_call(functools.partial(kernel, ring), out_shape=tuple((pltpu.VM...  115 us

profile of v4, /device:TPU:46, one launch (start us, length us, event | category | flops | bytes accessed | tf_op | source)
XLA Modules:
  0.0 116.4 jit_solution(4225875287254058480)
XLA Ops:
  0.6 114.7 %march.1 = (f32[128,8,128]{2,1,0:T(8,128)S(1)}, f32[4,256,128]{2,1,0:T(8,128)S(1)}) custom-call(f32[128,8,128]{2,1,0:T(8,128)} %pressure.1, f32[128,8,128]{2,1,0:T(8,128)} %prior.1, bf16[128,8,128]{2,1,0:T(8,128)(2,1)} %courant.1, f32[16]{0:T(128)} %wavelet.1, s32[8,128]{1,0:T(8,128)} %delay.1, s32[8,128]{1,0:T(8,128)} %source.1, s32[8,128]{1,0:T(8,128)} %receiver.1, ...), custom_call_target="tpu_custom_call" | custom-call | tf_op jit(solution)/shard_map/march/pallas_call | solution.py:348
  115.4 1.0 put.1

commit v5 on v4

--- a/solution.py
+++ b/solution.py
@@ -14,7 +14,7 @@
 ROWS = 32
 PAIRS = ROWS // 2
 GROUP = 4
-EARLY = 10
+EARLY = 12
 HEAD = 6
 MESH = pl.DeviceIdType.MESH
 
@@ -179,18 +179,22 @@
         a, b = from_left[now, c, i], from_right[now, c, i]
         return jnp.where(low, b, a), pltpu.roll(jnp.where(low, a, b), REACH, 0)
 
-    pl.semaphore_wait(barrier, 3)
-    tell()
-
     def open_chunk(c, _):
         load_chunk(c).wait()
         for i in range(PAIRS):
             z = c * ROWS + 2 * i + REACH
             pack(0, c, i, field[0, z], field[0, z + 1])
+        return 0
+
+    lax.fori_loop(0, chunks, open_chunk, 0)
+    pl.semaphore_wait(barrier, 3)
+
+    def open_send(c, _):
         send(0, c)
         return 0
 
-    lax.fori_loop(0, chunks, open_chunk, 0)
+    lax.fori_loop(0, chunks, open_send, 0)
+    tell()
 
     for load in loads:
         load.wait()

time: 116 us -> 116 us (level)
  no operation moved by 1% of the time
where the time goes in v5:
time: 116 us
  Pallas kernels  116 us (100%)
    pallas_call x1, Pallas kernels, shards(): pl.pallas_call(functools.partial(kernel, ring), out_shape=tuple((pltpu.VM...  115 us

profile of v5, /device:TPU:46, one launch (start us, length us, event | category | flops | bytes accessed | tf_op | source)
XLA Modules:
  0.0 116.3 jit_solution(10581300774922553897)
XLA Ops:
  0.6 114.7 %march.1 = (f32[128,8,128]{2,1,0:T(8,128)S(1)}, f32[4,256,128]{2,1,0:T(8,128)S(1)}) custom-call(f32[128,8,128]{2,1,0:T(8,128)} %pressure.1, f32[128,8,128]{2,1,0:T(8,128)} %prior.1, bf16[128,8,128]{2,1,0:T(8,128)(2,1)} %courant.1, f32[16]{0:T(128)} %wavelet.1, s32[8,128]{1,0:T(8,128)} %delay.1, s32[8,128]{1,0:T(8,128)} %source.1, s32[8,128]{1,0:T(8,128)} %receiver.1, ...), custom_call_target="tpu_custom_call" | custom-call | tf_op jit(solution)/shard_map/march/pallas_call | solution.py:352
  115.3 1.0 put.1

commit v6 on v5

--- a/solution.py
+++ b/solution.py
@@ -307,7 +307,7 @@
         key = half - 1 + HEAD - i
         for k, low_owner in ((key, False), (key - HEAD, True)):
             for owner in (lax.rem(me + k + ring, ring), lax.rem(me - k + ring, ring)):
-                @pl.when((k >= 1) & (k < half) & ((owner < ring // 8) == low_owner))
+                @pl.when((k >= 1) & (k < half) & ((owner < ring // 16) == low_owner))
                 def _():
                     send_block(owner)
 

time: 116 us -> 116 us (level)
  no operation moved by 1% of the time
where the time goes in v6:
time: 116 us
  Pallas kernels  115 us (99%)
    pallas_call x1, Pallas kernels, shards(): pl.pallas_call(functools.partial(kernel, ring), out_shape=tuple((pltpu.VM...  114 us

profile of v6, /device:TPU:46, one launch (start us, length us, event | category | flops | bytes accessed | tf_op | source)
XLA Modules:
  0.0 115.5 jit_solution(11663971560770248673)
XLA Ops:
  0.6 113.9 %march.1 = (f32[128,8,128]{2,1,0:T(8,128)S(1)}, f32[4,256,128]{2,1,0:T(8,128)S(1)}) custom-call(f32[128,8,128]{2,1,0:T(8,128)} %pressure.1, f32[128,8,128]{2,1,0:T(8,128)} %prior.1, bf16[128,8,128]{2,1,0:T(8,128)(2,1)} %courant.1, f32[16]{0:T(128)} %wavelet.1, s32[8,128]{1,0:T(8,128)} %delay.1, s32[8,128]{1,0:T(8,128)} %source.1, s32[8,128]{1,0:T(8,128)} %receiver.1, ...), custom_call_target="tpu_custom_call" | custom-call | tf_op jit(solution)/shard_map/march/pallas_call | solution.py:352
  114.6 1.0 put.1
